TPU v7x, 32 devices: a whole 2x2x4 slice. The times are simulated.
32 devices in a mesh: ctx: 8 (over y, x, core), tp: 4 (over z).
Axes of the slice: x: 2, y: 2, z: 4, core: 2. Of those that a mesh axis runs over, the one named last changes fastest.
Arguments:
- hidden_in: bfloat16 [2048, 4096], P(('ctx', 'tp')), may hold values from -6 to 6
- norm_gain: float32 [4096], replicated, may hold values from 0.5 to 1.5
- proj_weight: bfloat16 [4096, 4096], P(None, 'tp'), may hold values from -0.09375 to 0.09375
- conv_in: bfloat16 [2048, 4096], P('ctx', 'tp'), may hold values from -6 to 6
- conv_weight: float32 [4, 4096], P(None, 'tp'), may hold values from -3 to 3
- conv_bias: float32 [4096], P('tp'), may hold values from -3 to 3
- act_grad: bfloat16 [2048, 4096], P('ctx', 'tp'), may hold values from -6 to 6
Outputs:
- hidden_input_gradient: bfloat16 [2048, 4096], P(('ctx', 'tp'))
- norm_gain_gradient: float32 [4096], replicated
- taps_grad: float32 [4, 4096], P(None, 'tp')
- bias_grad: float32 [4096], P('tp')
All inputs are finite; a program needn't handle non-finite values.
Results may differ from a plain program's by a relative error of at most 0.013.
Values may be sent and summed in bfloat16 or wider, within the bound.
A program may use at most 64 MiB of HBM per device.

v0:
```python
import jax
import jax.numpy as jnp
from jax import lax
from jax.sharding import PartitionSpec as P


def from_behind(block, axis, distance):
    devices = range(lax.axis_size(axis))
    route = [(i - distance, i) for i in devices if i - distance in devices]
    return lax.ppermute(block, axis, route)


def preact_of(padded, taps, offset, count_tok):
    tap_count = taps.shape[0]
    return offset[None, :] + sum(
        (
            taps[index][None, :] * padded[tap_count - 1 - index : tap_count - 1 - index + count_tok]
            for index in range(tap_count)
        )
    )


def grad_of(preact, cotangent):
    sigmoid_v = jax.nn.sigmoid(preact)
    return cotangent.astype(jnp.float32) * sigmoid_v * (1.0 + preact * (1.0 - sigmoid_v))


def on_device(hidden_in, norm_gain, proj_weight, conv_in, conv_weight, conv_bias, act_grad):
    count_tok = conv_in.shape[0]
    tap_count = conv_weight.shape[0]
    edge_rows = tap_count - 1
    earlier = from_behind(conv_in[count_tok - edge_rows :], "ctx", 1)
    later_in, later_grad = from_behind((conv_in[:edge_rows], act_grad[:edge_rows]), "ctx", -1)
    padded = jnp.concatenate([earlier, conv_in], 0).astype(jnp.float32)
    preact = preact_of(padded, conv_weight, conv_bias, count_tok)
    pre_grad = grad_of(preact, act_grad)
    tail_pad = jnp.concatenate([conv_in[count_tok - edge_rows :], later_in], 0).astype(jnp.float32)
    tail_pre = preact_of(tail_pad, conv_weight, conv_bias, edge_rows)
    next_grad = grad_of(tail_pre, later_grad)
    taps_part = jnp.stack(
        [
            jnp.sum(pre_grad * padded[edge_rows - index : edge_rows - index + count_tok], 0)
            for index in range(tap_count)
        ],
        0,
    )
    bias_part = jnp.sum(pre_grad, 0)
    taps_grad, bias_grad = lax.psum((taps_part, bias_part), "ctx")
    after = jnp.concatenate([pre_grad, next_grad], 0)
    in_grad = sum(
        (
            conv_weight[index][None, :] * after[index : index + count_tok]
            for index in range(tap_count)
        )
    ).astype(jnp.bfloat16)
    whole_term = lax.dot_general(
        in_grad, proj_weight, (((1,), (1,)), ((), ())), preferred_element_type=jnp.float32
    )
    normalized_gradient = lax.psum_scatter(
        whole_term.astype(jnp.bfloat16), "tp", scatter_dimension=0, tiled=True
    ).astype(jnp.float32)
    hidden_state = hidden_in.astype(jnp.float32)
    root_mean_square = jnp.sqrt(jnp.mean(hidden_state * hidden_state, -1, keepdims=True) + 1e-05)
    normalized_input = hidden_state / root_mean_square
    norm_gain_gradient = lax.psum(jnp.sum(normalized_gradient * normalized_input, 0), ("ctx", "tp"))
    scaled_gradient = norm_gain[None, :] * normalized_gradient
    mean_correction = jnp.mean(scaled_gradient * normalized_input, -1, keepdims=True)
    hidden_input_gradient = (
        (scaled_gradient - normalized_input * mean_correction) / root_mean_square
    ).astype(jnp.bfloat16)
    return (hidden_input_gradient, norm_gain_gradient, taps_grad, bias_grad)


def solution(mesh):
    return jax.shard_map(
        on_device,
        mesh=mesh,
        in_specs=(
            P(("ctx", "tp"), None),
            P(),
            P(None, "tp"),
            P("ctx", "tp"),
            P(None, "tp"),
            P("tp"),
            P("ctx", "tp"),
        ),
        out_specs=(P(("ctx", "tp"), None), P(), P(None, "tp"), P("tp")),
        check_vma=False,
    )
```

profile of v0, /device:TPU:0, one launch (start us, length us, event | category | flops | bytes accessed | tf_op | source)
XLA Modules:
  0.0 122.8 jit_solution(8762573390390648197)
XLA Ops:
  7.2 0.0 copy-start.2
  7.2 0.0 copy-start.4
  7.2 0.0 reduce-scatter.2.cloned.1.call-start
  7.2 0.8 fusion.26
  8.0 2.4 %collective-permute-start = (bf16[3,1024]{1,0:T(4,128)(2,1)S(1)}, bf16[3,1024]{1,0:T(4,128)(2,1)S(1)}, u32[]{:S(2)}, u32[]{:S(2)}) collective-permute-start(bf16[3,1024]{1,0:T(4,128)(2,1)S(1)} %get-tuple-element.14), channel_id=1, source_target_pairs={{0,4},{4,8},{8,12},{12,16},{16,20},{20,24},{24,28},{1,5},{5,9},{9,... | collective-permute-start | bytes 18440 | tf_op jit(solution)/shard_map/ppermute | solution.py:10
  10.4 1.3 %collective-permute-start.2 = (bf16[3,1024]{1,0:T(4,128)(2,1)S(1)}, bf16[3,1024]{1,0:T(4,128)(2,1)S(1)}, u32[]{:S(2)}, u32[]{:S(2)}) collective-permute-start(bf16[3,1024]{1,0:T(4,128)(2,1)S(1)} %get-tuple-element.15), channel_id=1, source_target_pairs={{4,0},{8,4},{12,8},{16,12},{20,16},{24,20},{28,24},{5,1},{9,5},{13... | collective-permute-start | bytes 18440 | tf_op jit(solution)/shard_map/ppermute | solution.py:10
  11.7 0.7 slice.76
  12.5 1.3 %collective-permute-start.1 = (bf16[3,1024]{1,0:T(4,128)(2,1)S(1)}, bf16[3,1024]{1,0:T(4,128)(2,1)S(1)}, u32[]{:S(2)}, u32[]{:S(2)}) collective-permute-start(bf16[3,1024]{1,0:T(4,128)(2,1)S(1)} %slice.76), channel_id=1, source_target_pairs={{4,0},{8,4},{12,8},{16,12},{20,16},{24,20},{28,24},{5,1},{9,5},{13... | collective-permute-start | bytes 18440 | tf_op jit(solution)/shard_map/ppermute | solution.py:10
  13.7 0.9 fusion.27
  14.6 0.0 collective-permute-done
  14.6 1.2 maximum_convert_fusion
  15.8 0.0 copy-done.2
  15.8 0.0 copy-done.4
  15.9 1.3 %multiply_reduce_fusion.3 = (f32[1024]{0:T(1024)S(1)}, f32[1024]{0:T(1024)S(1)}, f32[1024]{0:T(1024)S(1)}, f32[1024]{0:T(1024)S(1)}, f32[1024]{0:T(1024)S(1)}, /*index=5*/f32[256,1024]{1,0:T(8,128)S(1)}) fusion(f32[259,1024]{1,0:T(8,128)S(1)} %maximum_convert_fusion, f32[1024]{0:T(1024)S(1)} %bitcast.15, f32[1024]{0:T(1024)S(1)} %bitcast.18, ...), kind=kLoop, calls=%fused_computation.27 | loop fusion | flops 6810624 | bytes 5808128 | tf_op jit(solution)/shard_map/reduce_sum | solution.py:42
  17.1 0.0 collective-permute-done.2
  17.2 1.1 collective-permute-done.1
  18.3 7.4 %convolution_convert_fusion = bf16[256,4096]{1,0:T(8,128)(2,1)} fusion(bf16[4096,1024]{1,0:T(8,128)(2,1)} %param.9, f32[3,1024]{1,0:T(4,128)S(1)} %add_multiply_fusion.1, f32[256,1024]{1,0:T(8,128)S(1)} %get-tuple-element.13, f32[1024]{0:T(1024)S(1)} %bitcast.17, f32[1024]{0:T(1024)S(1)} %bitcast.20, f32[1024]{0:T(1024)S(1)} %bitcast.14, f32[1024]{0:T(1024)S(1)} %bitcast.11), kind=kOutput, calls=%fused_computation | convolution fusion | flops 2151415808 | bytes 11563008 | tf_op jit(solution)/shard_map/dot_general | solution.py:56
  25.6 0.0 copy-start
  25.6 0.0 copy-start.3
  25.6 0.0 reduce-scatter.2.cloned.1.call-update
  25.7 1.0 copy-done
  26.7 0.2 fusion.6
  26.9 29.4 %all-reduce = (f32[4,1024]{1,0:T(4,128)}, f32[1024]{0:T(1024)}) all-reduce(f32[4,1024]{1,0:T(4,128)S(1)} %pad_maximum_fusion.1, f32[1024]{0:T(1024)S(1)} %get-tuple-element.10), channel_id=1, replica_groups=mesh['ctx'=8,'tp'=4] {'ctx'}, use_global_device_ids=true, to_apply=%region_9.0 | all-reduce | flops 5120 | bytes 40960 | tf_op jit(solution)/shard_map/psum | solution.py:48
  56.4 17.4 %reduce-scatter.2.cloned.1.call-done = bf16[64,4096]{1,0:T(8,128)(2,1)} async-done(((bf16[256,4096]{1,0:T(8,128)(2,1)}), bf16[64,4096]{1,0:T(8,128)(2,1)}) %reduce-scatter.2.cloned.1.call-update) | async-done | bytes 524304 | tf_op jit(solution)/shard_map/reduce_scatter | solution.py:59
  73.7 0.0 copy-done.3
  73.7 0.0 copy-start.1
  73.7 1.6 %fusion.5 = (f32[4096]{0:T(1024)S(1)}, f32[64]{0:T(128)S(1)}) fusion(bf16[64,4096]{1,0:T(8,128)(2,1)} %reduce-scatter.2.cloned.1.call-done, f32[64]{0:T(128)S(1)} %add_sqrt_fusion, bf16[64,4096]{1,0:T(8,128)(2,1)S(1)} %copy-done, f32[4096]{0:T(1024)S(1)} %copy-done.3), kind=kLoop, calls=%fused_computation.12 | loop fusion | flops 2092992 | bytes 1081856 | tf_op jit(solution)/shard_map/reduce_sum | solution.py:65
  75.3 39.5 %psum.21 = f32[4096]{0:T(1024)} all-reduce(f32[4096]{0:T(1024)S(1)} %get-tuple-element.8), channel_id=1, replica_groups=mesh['ctx'=8,'tp'=4] {'ctx','tp'}, use_global_device_ids=true, to_apply=%region_4.0 | all-reduce | flops 4096 | bytes 32768 | tf_op jit(solution)/shard_map/psum | solution.py:65
  114.8 0.0 copy-done.1
  114.8 1.1 fusion.4
  (5 shorter events, 0.1 us)
Async XLA Ops:
  7.2 8.7 %copy-start.2 = (bf16[256,1024]{1,0:T(8,128)(2,1)S(1)}, bf16[256,1024]{1,0:T(8,128)(2,1)}, u32[]{:S(2)}) copy-start(bf16[256,1024]{1,0:T(8,128)(2,1)} %param.13) | copy-start | bytes 1572868
  7.2 8.7 %copy-start.4 = (f32[1024]{0:T(1024)S(1)}, f32[1024]{0:T(1024)}, u32[]{:S(2)}) copy-start(f32[1024]{0:T(1024)} %param.12) | copy-start | bytes 12292
  7.2 66.6 %reduce-scatter.2.cloned.1.call-start = ((), (), s32[]{:S(2)}) async-start(), calls=%async_computation.1 | async-start | bytes 2621440 | tf_op jit(solution)/shard_map/reduce_scatter | solution.py:59
  8.0 6.6 %collective-permute-start = (bf16[3,1024]{1,0:T(4,128)(2,1)S(1)}, bf16[3,1024]{1,0:T(4,128)(2,1)S(1)}, u32[]{:S(2)}, u32[]{:S(2)}) collective-permute-start(bf16[3,1024]{1,0:T(4,128)(2,1)S(1)} %get-tuple-element.14), channel_id=1, source_target_pairs={{0,4},{4,8},{8,12},{12,16},{16,20},{20,24},{24,28},{1,5},{5,9},{9,... | collective-permute-start | bytes 18440 | tf_op jit(solution)/shard_map/ppermute | solution.py:10
  10.4 6.7 %collective-permute-start.2 = (bf16[3,1024]{1,0:T(4,128)(2,1)S(1)}, bf16[3,1024]{1,0:T(4,128)(2,1)S(1)}, u32[]{:S(2)}, u32[]{:S(2)}) collective-permute-start(bf16[3,1024]{1,0:T(4,128)(2,1)S(1)} %get-tuple-element.15), channel_id=1, source_target_pairs={{4,0},{8,4},{12,8},{16,12},{20,16},{24,20},{28,24},{5,1},{9,5},{13... | collective-permute-start | bytes 18440 | tf_op jit(solution)/shard_map/ppermute | solution.py:10
  12.5 5.8 %collective-permute-start.1 = (bf16[3,1024]{1,0:T(4,128)(2,1)S(1)}, bf16[3,1024]{1,0:T(4,128)(2,1)S(1)}, u32[]{:S(2)}, u32[]{:S(2)}) collective-permute-start(bf16[3,1024]{1,0:T(4,128)(2,1)S(1)} %slice.76), channel_id=1, source_target_pairs={{4,0},{8,4},{12,8},{16,12},{20,16},{24,20},{28,24},{5,1},{9,5},{13... | collective-permute-start | bytes 18440 | tf_op jit(solution)/shard_map/ppermute | solution.py:10
  25.6 1.0 copy-start
  25.6 48.1 %copy-start.3 = (f32[4096]{0:T(1024)S(1)}, f32[4096]{0:T(1024)}, u32[]{:S(2)}) copy-start(f32[4096]{0:T(1024)} %param.8) | copy-start | bytes 49156
  73.7 41.1 %copy-start.1 = (bf16[64,4096]{1,0:T(8,128)(2,1)S(1)}, bf16[64,4096]{1,0:T(8,128)(2,1)}, u32[]{:S(2)}) copy-start(bf16[64,4096]{1,0:T(8,128)(2,1)} %reduce-scatter.2.cloned.1.call-done) | copy-start | bytes 1572868
Sparse Core Ops, SparseCore 0:
  25.8 47.9 reduce-scatter.1
where the time goes:
time: 123 us
  blocking collectives  68.9 us (56%)
  waiting for transfers between devices  18.5 us (15%)
  between operations  14.1 us (11%)
  matrix products  7.36 us (6%)
  other arithmetic  5.41 us (4%)
  starting transfers between devices  5.01 us (4%)
  local copies, waits for them, and re-layouts  3.44 us (3%)
    psum x1, blocking collectives, on_device(): lax.psum(jnp.sum(normalized_gradient * normalized_input, 0), ('ctx', 'tp'))  39.5 us
    psum x1, blocking collectives, on_device(): taps_grad, bias_grad = lax.psum((taps_part, bias_part), 'ctx')  29.4 us
    reduce_scatter x1, waiting for transfers between devices, on_device(): lax.psum_scatter(whole_term.astype(jnp.bfloat16), 'tp', scatter_dimension...  17.4 us
    dot_general x1, matrix products, on_device(): lax.dot_general(in_grad, proj_weight, (((1,), (1,)), ((), ())), preferred...  7.36 us
    ppermute x3, starting transfers between devices, from_behind(): return lax.ppermute(block, axis, route)  4.97 us
  transfers between devices with their start and end apart: 4, of which 2 were waited for; matrix products, arithmetic and copies ran while one was open for 4% of the time, Pallas kernels for 0%

commit v1 on v0

v1 whole, which is shorter than its diff:
```python
import functools

import jax
import jax.numpy as jnp
from jax import lax
from jax.experimental import pallas as pl
from jax.experimental.pallas import tpu as pltpu
from jax.sharding import PartitionSpec as P

MESH = pl.DeviceIdType.MESH
F32 = jnp.float32
BF16 = jnp.bfloat16
LANES = 128
EDGE = 16
PAD = 8


def chunk_of(rows, most=64):
    return max(r for r in range(EDGE, most + 1, EDGE) if rows % r == 0)


def each(count, body):
    if count <= 8:
        for k in range(1, count):
            body(k)
    else:
        lax.fori_loop(1, count, lambda k, _: (body(k), 0)[1], 0)


def kernel(
    n_ctx, n_tp, slab_w,
    hid_hbm, gain_ref, w_hbm, x_hbm, taps_ref, bias_ref, g_hbm,
    out_hbm, gain_out, taps_out, bias_out,
    hid_v, w_v, x_v, g_v, halo, xf, pg, act, tb, prod, send, recv,
    xh, ng, inv_v, out_v, tb_all, gain_all, gain_tp,
    in_sem, w_sem, out_sem, halo_send, halo_recv, rs_send, rs_recv,
    tb_send, tb_recv, gc_send, gc_recv, gt_send, gt_recv,
):
    ctx = lax.axis_index("ctx")
    tp = lax.axis_index("tp")
    T, C = x_v.shape
    D = w_v.shape[0]
    taps = taps_ref.shape[0]
    rows = T // n_tp
    half = n_tp // 2
    slabs = D // slab_w
    prev_c, next_c = lax.rem(ctx + n_ctx - 1, n_ctx), lax.rem(ctx + 1, n_ctx)
    ring = (lax.rem(tp + 1, n_tp), lax.rem(tp + n_tp - 1, n_tp))

    barrier = pltpu.get_barrier_semaphore()

    def greet_ctx(k):
        pl.semaphore_signal(barrier, inc=1, device_id={"ctx": lax.rem(ctx + k, n_ctx)}, device_id_type=MESH)

    def greet_tp(k):
        pl.semaphore_signal(barrier, inc=1, device_id={"tp": lax.rem(tp + k, n_tp)}, device_id_type=MESH)

    each(n_ctx, greet_ctx)
    each(n_tp, greet_tp)

    x_in = pltpu.make_async_copy(x_hbm, x_v, in_sem.at[0])
    g_in = pltpu.make_async_copy(g_hbm, g_v, in_sem.at[1])
    h_in = pltpu.make_async_copy(hid_hbm, hid_v, in_sem.at[2])
    x_in.start()
    g_in.start()

    def w_copy(j):
        part = pl.ds(pl.multiple_of(j * slab_w, slab_w), slab_w)
        return pltpu.make_async_copy(w_hbm.at[part], w_v.at[part], w_sem.at[j])

    for j in range(slabs):
        w_copy(j).start()
    h_in.start()

    pl.semaphore_wait(barrier, n_ctx + n_tp - 2)

    def remote(src, dst, s_sem, r_sem, **where):
        return pltpu.make_async_remote_copy(
            src_ref=src, dst_ref=dst, send_sem=s_sem, recv_sem=r_sem,
            device_id=where, device_id_type=MESH,
        )

    halos = [
        remote(x_hbm.at[pl.ds(T - EDGE, EDGE)], halo.at[0], halo_send.at[0], halo_recv.at[0], ctx=next_c),
        remote(x_hbm.at[pl.ds(0, EDGE)], halo.at[1], halo_send.at[1], halo_recv.at[1], ctx=prev_c),
        remote(g_hbm.at[pl.ds(0, EDGE)], halo.at[2], halo_send.at[2], halo_recv.at[2], ctx=prev_c),
    ]
    for copy in halos:
        copy.start()

    x_in.wait()
    g_in.wait()

    def fold(v):
        return v.reshape(v.shape[0] // 8, 8, v.shape[1]).sum(0)

    def grad_rows(t0, count, cols, cot):
        xs = [xf[pl.ds(PAD + t0 - k, count), cols] for k in range(taps)]
        pre = bias_ref[:, cols] + sum(taps_ref[pl.ds(k, 1), cols] * xs[k] for k in range(taps))
        s = 0.5 * jnp.tanh(0.5 * pre) + 0.5
        return xs, cot.astype(F32) * s * (1.0 + pre * (1.0 - s))

    def in_rows(t0, count, cols):
        total = sum(taps_ref[pl.ds(k, 1), cols] * pg[pl.ds(t0 + k, count), cols] for k in range(taps))
        act[pl.ds(t0, count), cols] = total.astype(BF16)

    def columns(c):
        return pl.ds(pl.multiple_of(c * LANES, LANES), LANES)

    step = chunk_of(T - EDGE)
    step_in = chunk_of(T - 2 * EDGE)
    tb[...] = jnp.zeros_like(tb)

    def interior(c, _):
        cols = columns(c)
        xf[pl.ds(PAD, T), cols] = x_v[:, cols].astype(F32)
        sums = [jnp.zeros((8, LANES), F32) for _ in range(taps + 1)]
        for t0 in range(EDGE, T, step):
            xs, g = grad_rows(t0, step, cols, g_v[pl.ds(t0, step), cols])
            pg[pl.ds(t0, step), cols] = g
            for k in range(taps):
                sums[k] += fold(g * xs[k])
            sums[taps] += fold(g)
        for k in range(taps + 1):
            tb[pl.ds(k, 1), cols] = jnp.sum(sums[k], 0, keepdims=True)
        for t0 in range(EDGE, T - EDGE, step_in):
            in_rows(t0, step_in, cols)
        return 0

    lax.fori_loop(0, C // LANES, interior, 0)

    for copy in halos:
        copy.wait_recv()
    has_prev = (ctx > 0).astype(F32)
    has_next = (ctx < n_ctx - 1).astype(F32)

    def edges(c, _):
        cols = columns(c)
        xf[pl.ds(0, PAD), cols] = halo[0, :, cols].astype(F32)[EDGE - PAD:] * has_prev
        xf[pl.ds(PAD + T, PAD), cols] = halo[1, :, cols].astype(F32)[:PAD]
        xs, g = grad_rows(0, EDGE, cols, g_v[pl.ds(0, EDGE), cols])
        pg[pl.ds(0, EDGE), cols] = g
        for k in range(taps):
            tb[pl.ds(k, 1), cols] += jnp.sum(fold(g * xs[k]), 0, keepdims=True)
        tb[pl.ds(taps, 1), cols] += jnp.sum(fold(g), 0, keepdims=True)
        _, after = grad_rows(T, PAD, cols, halo[2, :, cols].astype(F32)[:PAD])
        pg[pl.ds(T, PAD), cols] = after * has_next
        in_rows(0, EDGE, cols)
        in_rows(T - EDGE, EDGE, cols)
        return 0

    lax.fori_loop(0, C // LANES, edges, 0)

    tb_all[ctx] = tb[...]

    def tb_copy(k):
        return remote(
            tb_all.at[ctx], tb_all.at[ctx], tb_send.at[k], tb_recv.at[ctx],
            ctx=lax.rem(ctx + k, n_ctx),
        )

    def owner(d, s):
        away = half - s
        return lax.rem(tp + (away if d == 0 else n_tp - away), n_tp)

    def rs_copy(d, s, j):
        return remote(
            send.at[d, s, j], recv.at[d, s, j], rs_send.at[d, s, j], rs_recv.at[d, s, j],
            tp=ring[d],
        )

    def term(d, s, j):
        return prod[j, pl.ds(pl.multiple_of(owner(d, s) * rows, rows), rows), :]

    def first_sends(pair, _):
        for d in range(2):
            j = 2 * pair + d
            w_copy(j).wait()
            part = pl.ds(pl.multiple_of(j * slab_w, slab_w), slab_w)
            prod[j] = lax.dot_general(
                act[...], w_v[part, :], (((1,), (1,)), ((), ())), preferred_element_type=F32
            )
            send[d, 0, j] = term(d, 0, j).astype(BF16)
            rs_copy(d, 0, j).start()
            send[1 - d, 1, j] = term(1 - d, 1, j).astype(BF16)
            rs_copy(1 - d, 1, j).start()
        return 0

    lax.fori_loop(0, slabs // 2, first_sends, 0)
    each(n_ctx, lambda k: tb_copy(k).start())

    h_in.wait()

    def slab_cols(j):
        return pl.ds(pl.multiple_of(j * slab_w, slab_w), slab_w)

    def fold_lanes(v):
        return sum(v[:, i:i + LANES] for i in range(0, v.shape[1], LANES))

    def squares(j, acc):
        h = hid_v[:, slab_cols(j)].astype(F32)
        return acc + fold_lanes(h * h)

    acc = lax.fori_loop(0, slabs, squares, jnp.zeros((rows, LANES), F32))
    inv = lax.rsqrt(jnp.sum(acc, -1, keepdims=True) / D + 1e-05)
    inv_v[...] = jnp.broadcast_to(inv, (rows, LANES))

    def second_sends(pair, _):
        for d in range(2):
            j = 2 * pair + d
            rs_copy(d, 0, j).wait_recv()
            send[d, 1, j] = (term(d, 1, j) + recv[d, 0, j].astype(F32)).astype(BF16)
            rs_copy(d, 1, j).start()
        return 0

    lax.fori_loop(0, slabs // 2, second_sends, 0)

    for s in range(2, half):
        def later_sends(j, _, s=s):
            for d in range(2):
                rs_copy(d, s - 1, j).wait_recv()
                send[d, s, j] = (term(d, s, j) + recv[d, s - 1, j].astype(F32)).astype(BF16)
                rs_copy(d, s, j).start()
            return 0

        lax.fori_loop(0, slabs, later_sends, 0)

    def normalise(j, _):
        xh[j] = hid_v[:, slab_cols(j)].astype(F32) * inv_v[:, :1]
        return 0

    lax.fori_loop(0, slabs, normalise, 0)

    each(n_ctx, lambda k: remote(
        tb_all.at[ctx], tb_all.at[lax.rem(ctx + k, n_ctx)], tb_send.at[k],
        tb_recv.at[lax.rem(ctx + k, n_ctx)], ctx=next_c,
    ).wait_recv())
    total = lax.fori_loop(1, n_ctx, lambda i, t: t + tb_all[i], tb_all[0])
    taps_out[...] = total[:taps]
    bias_out[...] = total[taps:taps + 1]

    last = half - 1

    def finish(j, macc):
        rs_copy(0, last, j).wait_recv()
        rs_copy(1, last, j).wait_recv()
        mine = prod[j, pl.ds(pl.multiple_of(tp * rows, rows), rows), :]
        v = mine + recv[0, last, j].astype(F32) + recv[1, last, j].astype(F32)
        ng[j] = v
        vx = v * xh[j]
        gain_all[ctx, pl.ds(j, 1), :] = jnp.sum(fold(vx), 0, keepdims=True)
        return macc + fold_lanes(vx * gain_ref[:, slab_cols(j)])

    macc = lax.fori_loop(0, slabs, finish, jnp.zeros((rows, LANES), F32))

    def gc_copy(k, slot):
        return remote(
            gain_all.at[slot], gain_all.at[slot], gc_send.at[k], gc_recv.at[slot],
            ctx=lax.rem(ctx + k, n_ctx),
        )

    each(n_ctx, lambda k: gc_copy(k, ctx).start())

    mean = jnp.sum(macc, -1, keepdims=True) / D

    def write(j, _):
        cols = slab_cols(j)
        res = (gain_ref[:, cols] * ng[j] - xh[j] * mean) * inv_v[:, :1]
        out_v[:, cols] = res.astype(BF16)
        return 0

    lax.fori_loop(0, slabs, write, 0)
    out_copy = pltpu.make_async_copy(out_v, out_hbm, out_sem)
    out_copy.start()

    each(n_ctx, lambda k: gc_copy(k, lax.rem(ctx + k, n_ctx)).wait_recv())
    gain_tp[tp] = lax.fori_loop(1, n_ctx, lambda i, t: t + gain_all[i], gain_all[0])

    def gt_copy(k, slot):
        return remote(
            gain_tp.at[slot], gain_tp.at[slot], gt_send.at[k], gt_recv.at[slot],
            tp=lax.rem(tp + k, n_tp),
        )

    each(n_tp, lambda k: gt_copy(k, tp).start())

    for copy in halos:
        copy.wait_send()
    each(n_ctx, lambda k: tb_copy(k).wait_send())
    each(n_ctx, lambda k: gc_copy(k, ctx).wait_send())

    def drain(pair, _):
        for d in range(2):
            rs_copy(d, 0, 2 * pair + d).wait_send()
            for s in range(1, half):
                rs_copy(d, s, 2 * pair).wait_send()
                rs_copy(d, s, 2 * pair + 1).wait_send()
        return 0

    lax.fori_loop(0, slabs // 2, drain, 0)

    each(n_tp, lambda k: gt_copy(k, lax.rem(tp + k, n_tp)).wait_recv())
    gain_sum = sum(gain_tp[i] for i in range(n_tp))
    for j in range(slabs):
        gain_out[:, j * slab_w:(j + 1) * slab_w] = gain_sum[j:j + 1]
    each(n_tp, lambda k: gt_copy(k, tp).wait_send())
    out_copy.wait()


def on_device(n_ctx, n_tp, hidden_in, norm_gain, proj_weight, conv_in, conv_weight, conv_bias, act_grad):
    T, C = conv_in.shape
    D = proj_weight.shape[0]
    rows = hidden_in.shape[0]
    taps = conv_weight.shape[0]
    half = n_tp // 2
    slab_w = D // 8
    slabs = D // slab_w
    hbm = pl.BlockSpec(memory_space=pl.ANY)
    vmem = pl.BlockSpec(memory_space=pltpu.VMEM)
    dma = pltpu.SemaphoreType.DMA
    grad, gain, taps_grad, bias_grad = pl.pallas_call(
        functools.partial(kernel, n_ctx, n_tp, slab_w),
        out_shape=(
            jax.ShapeDtypeStruct((rows, D), BF16),
            jax.ShapeDtypeStruct((1, D), F32),
            jax.ShapeDtypeStruct((taps, C), F32),
            jax.ShapeDtypeStruct((1, C), F32),
        ),
        in_specs=[hbm, vmem, hbm, hbm, vmem, vmem, hbm],
        out_specs=(hbm, vmem, vmem, vmem),
        scratch_shapes=[
            pltpu.VMEM((rows, D), BF16),
            pltpu.VMEM((D, C), BF16),
            pltpu.VMEM((T, C), BF16),
            pltpu.VMEM((T, C), BF16),
            pltpu.VMEM((3, EDGE, C), BF16),
            pltpu.VMEM((T + 2 * PAD, C), F32),
            pltpu.VMEM((T + PAD, C), F32),
            pltpu.VMEM((T, C), BF16),
            pltpu.VMEM((8, C), F32),
            pltpu.VMEM((slabs, T, slab_w), F32),
            pltpu.VMEM((2, half, slabs, rows, slab_w), BF16),
            pltpu.VMEM((2, half, slabs, rows, slab_w), BF16),
            pltpu.VMEM((slabs, rows, slab_w), F32),
            pltpu.VMEM((slabs, rows, slab_w), F32),
            pltpu.VMEM((rows, LANES), F32),
            pltpu.VMEM((rows, D), BF16),
            pltpu.VMEM((n_ctx, 8, C), F32),
            pltpu.VMEM((n_ctx, slabs, slab_w), F32),
            pltpu.VMEM((n_tp, slabs, slab_w), F32),
            dma((3,)),
            dma((slabs,)),
            dma,
            dma((3,)),
            dma((3,)),
            dma((2, half, slabs)),
            dma((2, half, slabs)),
            dma((n_ctx,)),
            dma((n_ctx,)),
            dma((n_ctx,)),
            dma((n_ctx,)),
            dma((n_tp,)),
            dma((n_tp,)),
        ],
        compiler_params=pltpu.CompilerParams(
            collective_id=0, has_side_effects=True, vmem_limit_bytes=60 * 1024 * 1024
        ),
    )(
        hidden_in, norm_gain[None, :], proj_weight, conv_in, conv_weight, conv_bias[None, :], act_grad
    )
    return grad, gain.reshape(-1), taps_grad, bias_grad.reshape(-1)


def solution(mesh):
    return jax.shard_map(
        functools.partial(on_device, mesh.shape["ctx"], mesh.shape["tp"]),
        mesh=mesh,
        in_specs=(
            P(("ctx", "tp"), None),
            P(),
            P(None, "tp"),
            P("ctx", "tp"),
            P(None, "tp"),
            P("tp"),
            P("ctx", "tp"),
        ),
        out_specs=(P(("ctx", "tp"), None), P(), P(None, "tp"), P("tp")),
        check_vma=False,
    )
```

time: 123 us -> 62.8 us (0.51)
  blocking collectives: 68.9 us -> 0 us
  Pallas kernels: 0 us -> 55.8 us
  waiting for transfers between devices: 18.5 us -> 0 us
  between operations: 14.1 us -> 0.64 us
  matrix products: 7.36 us -> 0 us
  other arithmetic: 5.41 us -> 0 us
  starting transfers between devices: 5.01 us -> 0 us
  local copies, waits for them, and re-layouts: 3.44 us -> 5.78 us
    psum x2 -> x0, blocking collectives: 68.9 us -> none  [the longest x1 39.5 us: on_device(): lax.psum(jnp.sum(normalized_gradient * normalized_input, 0), ('ctx', 'tp'))]
    pallas_call x0 -> x1, Pallas kernels: none -> 55.8 us  [on_device(): pl.pallas_call(functools.partial(kernel, n_ctx, n_tp, slab_w), out_shape=...]
    reduce_scatter x1 -> x0, waiting for transfers between devices: 17.4 us -> none  [on_device(): lax.psum_scatter(whole_term.astype(jnp.bfloat16), 'tp', scatter_dimension...]
    dot_general x1 -> x0, matrix products: 7.36 us -> none  [on_device(): lax.dot_general(in_grad, proj_weight, (((1,), (1,)), ((), ())), preferred...]
    ppermute x3 -> x0, starting transfers between devices: 4.97 us -> none  [from_behind(): return lax.ppermute(block, axis, route)]
    unnamed x10 -> x4, local copies, waits for them, and re-layouts: 1.03 us -> 5.78 us
    reduce_sum x3 -> x0, other arithmetic: 3.04 us -> none  [the longest x1 1.57 us: on_device(): jnp.sum(normalized_gradient * normalized_input, 0)]
    slice x3 -> x0, local copies, waits for them, and re-layouts: 2.4 us -> none  [the longest x1 0.89 us: on_device(): conv_weight[index][None, :] * after[index:index + count_tok]]
  transfers between devices with their start and end apart: 4 -> 0, of which waited for: 2 -> 0; matrix products, arithmetic and copies ran while one was open for 4% -> 0% of each run, Pallas kernels for 0% -> 0%
where the time goes in v1:
time: 62.8 us; the launch traced here: 62.3 us
  Pallas kernels  55.8 us (89%)
  local copies, waits for them, and re-layouts  5.78 us (9%)
  between operations  0.64 us (1%)
    pallas_call x1, Pallas kernels, on_device(): pl.pallas_call(functools.partial(kernel, n_ctx, n_tp, slab_w), out_shape=...  55.8 us
    unnamed x4, local copies, waits for them, and re-layouts  5.78 us

profile of v1, /device:TPU:0, one launch (start us, length us, event | category | flops | bytes accessed | tf_op | source)
XLA Modules:
  0.0 62.3 jit_solution(16851341262832590435)
XLA Ops:
  0.6 55.8 %shard_map.102 = (bf16[64,4096]{1,0:T(8,128)(2,1)}, f32[1,4096]{1,0:T(1,128)}, f32[4,1024]{1,0:T(4,128)}, f32[1,1024]{1,0:T(1,128)}) custom-call(bf16[64,4096]{1,0:T(8,128)(2,1)} %hid_hbm.1, f32[1,4096]{1,0:T(1,128)} %bitcast.4, bf16[4096,1024]{1,0:T(8,128)(2,1)} %w_hbm.1, bf16[256,1024]{1,0:T(8,128)(2,1)} %x_hbm.1, f32[4,1024]{1,0:T(4,128)} %taps_ref.1, ...), custom_call_target="tpu_custom_call" | custom-call | tf_op jit(solution)/shard_map/pallas_call | solution.py:321
  56.5 1.9 %copy.15 = bf16[64,4096]{1,0:T(8,128)(2,1)} copy(bf16[64,4096]{1,0:T(8,128)(2,1)} %get-tuple-element.16) | data formatting | bytes 1048576
  58.4 1.3 %copy.16 = f32[4096]{0:T(1024)} copy(f32[4096]{0:T(1024)} %bitcast.5) | data formatting | bytes 32768
  59.7 1.3 %copy.17 = f32[4,1024]{1,0:T(4,128)} copy(f32[4,1024]{1,0:T(4,128)} %get-tuple-element.18) | data formatting | bytes 32768
  61.0 1.3 %copy.18 = f32[1024]{0:T(1024)} copy(f32[1024]{0:T(1024)} %bitcast.7) | data formatting | bytes 8192

commit v2 on v1

v2 whole, which is shorter than its diff:
```python
import functools

import jax
import jax.numpy as jnp
from jax import lax
from jax.experimental import pallas as pl
from jax.experimental.pallas import tpu as pltpu
from jax.sharding import PartitionSpec as P

MESH = pl.DeviceIdType.MESH
F32 = jnp.float32
BF16 = jnp.bfloat16
LANES = 128
EDGE = 16
PAD = 8


def chunk_of(rows, most=64):
    return max(r for r in range(EDGE, most + 1, EDGE) if rows % r == 0)


def each(count, body):
    if count <= 8:
        for k in range(1, count):
            body(k)
    else:
        lax.fori_loop(1, count, lambda k, _: (body(k), 0)[1], 0)


def kernel(
    n_ctx, n_tp, slab_w,
    hid_hbm, gain_hbm, w_hbm, x_hbm, taps_hbm, bias_hbm, g_hbm,
    out_hbm, gain_out, taps_out, bias_out,
    hid_v, w_v, x_v, g_v, gain_ref, taps_ref, bias_ref, halo, xf, pg, act_mid, act_edge, tb, prod, send, recv,
    xh, ng, inv_v, out_v, tb_all, gain_all, gain_tp,
    in_sem, w_sem, out_sem, halo_send, halo_recv, rs_send, rs_recv,
    tb_send, tb_recv, gc_send, gc_recv, gt_send, gt_recv,
):
    ctx = lax.axis_index("ctx")
    tp = lax.axis_index("tp")
    T, C = x_v.shape
    D = w_v.shape[0]
    taps = taps_ref.shape[0]
    rows = T // n_tp
    slabs = D // slab_w
    groups, _, per_group, _ = gain_all.shape
    prev_c, next_c = lax.rem(ctx + n_ctx - 1, n_ctx), lax.rem(ctx + 1, n_ctx)
    line = (lax.rem(tp + 1, n_tp), lax.rem(tp + n_tp - 1, n_tp))

    barrier = pltpu.get_barrier_semaphore()

    def greet_ctx(k):
        pl.semaphore_signal(barrier, inc=1, device_id={"ctx": lax.rem(ctx + k, n_ctx)}, device_id_type=MESH)

    def greet_tp(k):
        pl.semaphore_signal(barrier, inc=1, device_id={"tp": lax.rem(tp + k, n_tp)}, device_id_type=MESH)

    each(n_ctx, greet_ctx)
    each(n_tp, greet_tp)

    inputs = [
        pltpu.make_async_copy(src, dst, in_sem.at[i])
        for i, (src, dst) in enumerate([
            (x_hbm, x_v), (taps_hbm, taps_ref), (bias_hbm, bias_ref), (g_hbm, g_v),
            (hid_hbm, hid_v), (gain_hbm, gain_ref),
        ])
    ]
    for copy in inputs[:4]:
        copy.start()

    def w_copy(j):
        part = pl.ds(pl.multiple_of(j * slab_w, slab_w), slab_w)
        return pltpu.make_async_copy(w_hbm.at[part], w_v.at[part], w_sem.at[j])

    for j in range(slabs):
        w_copy(j).start()
    for copy in inputs[4:]:
        copy.start()

    def remote(src, dst, s_sem, r_sem, **where):
        return pltpu.make_async_remote_copy(
            src_ref=src, dst_ref=dst, send_sem=s_sem, recv_sem=r_sem,
            device_id=where, device_id_type=MESH,
        )

    def fold(v):
        return v.reshape(v.shape[0] // 8, 8, v.shape[1]).sum(0)

    def convert(t0, count, cols):
        xf[pl.ds(PAD + t0, count), cols] = x_v[pl.ds(t0, count), cols].astype(F32)

    def grad_rows(t0, count, cols, cot):
        pre = bias_ref[:, cols] + sum(
            taps_ref[pl.ds(k, 1), cols] * xf[pl.ds(PAD + t0 - k, count), cols] for k in range(taps)
        )
        s = 0.5 * jnp.tanh(0.5 * pre) + 0.5
        return cot.astype(F32) * s * (1.0 + pre * (1.0 - s))

    def own_grad(first, stop, cols):
        step = chunk_of(stop - first)
        for t0 in range(first, stop, step):
            pg[pl.ds(t0, step), cols] = grad_rows(t0, step, cols, g_v[pl.ds(t0, step), cols])

    def in_rows(dst, at, first, count, cols):
        step = chunk_of(count)
        for i in range(0, count, step):
            total = sum(
                taps_ref[pl.ds(k, 1), cols] * pg[pl.ds(first + i + k, step), cols] for k in range(taps)
            )
            dst[pl.ds(at + i, step), cols] = total.astype(BF16)

    def columns(c):
        return pl.ds(pl.multiple_of(c * LANES, LANES), LANES)

    for copy in inputs[:4]:
        copy.wait()

    def middle(c, _):
        cols = columns(c)
        convert(rows - EDGE, T - 2 * rows + 2 * EDGE, cols)
        own_grad(rows, T - rows + EDGE, cols)
        in_rows(act_mid, 0, rows, T - 2 * rows, cols)
        return 0

    lax.fori_loop(0, C // LANES, middle, 0)

    pl.semaphore_wait(barrier, n_ctx + n_tp - 2)
    halos = [
        remote(x_hbm.at[pl.ds(T - EDGE, EDGE)], halo.at[0], halo_send.at[0], halo_recv.at[0], ctx=next_c),
        remote(x_hbm.at[pl.ds(0, EDGE)], halo.at[1], halo_send.at[1], halo_recv.at[1], ctx=prev_c),
        remote(g_hbm.at[pl.ds(0, EDGE)], halo.at[2], halo_send.at[2], halo_recv.at[2], ctx=prev_c),
    ]
    for copy in halos:
        copy.start()

    up = [n_tp - 2, n_tp - 1] + list(range(n_tp - 3, 0, -1))
    chunk = (up, [n_tp - 1 - r for r in up])
    begins = (tp == 0, tp == n_tp - 1)

    def sends(d, r):
        return tp < r if d == 0 else tp > r

    def rs_copy(d, r, j):
        return remote(
            send.at[d, r, j], recv.at[d, r, j], rs_send.at[d, r, j], rs_recv.at[d, r, j],
            tp=line[d],
        )

    def term(r, j):
        return prod[j, pl.ds(r * rows, rows), :]

    def begin(p, j):
        for d in range(2):
            r = chunk[d][p]

            @pl.when(begins[d])
            def _():
                send[d, r, j] = term(r, j).astype(BF16)
                rs_copy(d, r, j).start()

    def dot(a, j):
        part = pl.ds(pl.multiple_of(j * slab_w, slab_w), slab_w)
        return lax.dot_general(
            a[...], w_v[part, :], (((1,), (1,)), ((), ())), preferred_element_type=F32
        )

    def middle_dot(j, _):
        w_copy(j).wait()
        prod[j, pl.ds(rows, T - 2 * rows), :] = dot(act_mid, j)
        begin(0, j)
        return 0

    lax.fori_loop(0, slabs, middle_dot, 0)

    for copy in halos:
        copy.wait_recv()
    has_prev = (ctx > 0).astype(F32)
    has_next = (ctx < n_ctx - 1).astype(F32)

    def edges(c, _):
        cols = columns(c)
        xf[pl.ds(0, PAD), cols] = halo[0, :, cols].astype(F32)[EDGE - PAD:] * has_prev
        xf[pl.ds(PAD + T, PAD), cols] = halo[1, :, cols].astype(F32)[:PAD]
        convert(0, rows - EDGE, cols)
        convert(T - rows + EDGE, rows - EDGE, cols)
        own_grad(0, rows, cols)
        own_grad(T - rows + EDGE, T, cols)
        pg[pl.ds(T, PAD), cols] = has_next * grad_rows(T, PAD, cols, halo[2, :, cols].astype(F32)[:PAD])
        in_rows(act_edge, 0, 0, rows, cols)
        in_rows(act_edge, rows, T - rows, rows, cols)
        return 0

    lax.fori_loop(0, C // LANES, edges, 0)

    def edge_dot(j, _):
        both = dot(act_edge, j)
        prod[j, pl.ds(0, rows), :] = both[:rows]
        prod[j, pl.ds(T - rows, rows), :] = both[rows:]
        begin(1, j)
        return 0

    lax.fori_loop(0, slabs, edge_dot, 0)

    def later_begin(j, _, p=2):
        begin(p, j)
        return 0

    for p in range(2, n_tp - 1):
        lax.fori_loop(0, slabs, functools.partial(later_begin, p=p), 0)

    tb[...] = jnp.zeros_like(tb)

    def taps_terms(c, _):
        cols = columns(c)
        sums = [jnp.zeros((8, LANES), F32) for _ in range(taps + 1)]
        step = chunk_of(T)
        for t0 in range(0, T, step):
            g = pg[pl.ds(t0, step), cols]
            for k in range(taps):
                sums[k] += fold(g * xf[pl.ds(PAD + t0 - k, step), cols])
            sums[taps] += fold(g)
        for k in range(taps + 1):
            tb[pl.ds(k, 1), cols] = jnp.sum(sums[k], 0, keepdims=True)
        return 0

    lax.fori_loop(0, C // LANES, taps_terms, 0)
    tb_all[ctx] = tb[...]

    def tb_copy(k, slot):
        return remote(
            tb_all.at[slot], tb_all.at[slot], tb_send.at[k], tb_recv.at[slot],
            ctx=lax.rem(ctx + k, n_ctx),
        )

    each(n_ctx, lambda k: tb_copy(k, ctx).start())

    for copy in inputs[4:]:
        copy.wait()

    def slab_cols(j):
        return pl.ds(pl.multiple_of(j * slab_w, slab_w), slab_w)

    def fold_lanes(v):
        return sum(v[:, i:i + LANES] for i in range(0, v.shape[1], LANES))

    def squares(j, acc):
        h = hid_v[:, slab_cols(j)].astype(F32)
        return acc + fold_lanes(h * h)

    acc = lax.fori_loop(0, slabs, squares, jnp.zeros((rows, LANES), F32))
    inv = lax.rsqrt(jnp.sum(acc, -1, keepdims=True) / D + 1e-05)
    inv_v[...] = jnp.broadcast_to(inv, (rows, LANES))

    def normalise(j, _):
        xh[j] = hid_v[:, slab_cols(j)].astype(F32) * inv_v[:, :1]
        return 0

    lax.fori_loop(0, slabs, normalise, 0)

    def forward(j, _, p=0):
        def one(d):
            r = chunk[d][p]

            @pl.when(sends(d, r) & jnp.logical_not(begins[d]))
            def _():
                rs_copy(d, r, j).wait_recv()
                send[d, r, j] = (term(r, j) + recv[d, r, j].astype(F32)).astype(BF16)
                rs_copy(d, r, j).start()

        one(0)
        one(1)
        return 0

    for p in range(n_tp - 1):
        lax.fori_loop(0, slabs, functools.partial(forward, p=p), 0)

    each(n_ctx, lambda k: tb_copy(k, lax.rem(ctx + k, n_ctx)).wait_recv())
    total = lax.fori_loop(1, n_ctx, lambda i, t: t + tb_all[i], tb_all[0])
    taps_out[...] = total[:taps]
    bias_out[...] = total[taps:taps + 1]

    def gc_copy(g, k, slot):
        return remote(
            gain_all.at[g, slot], gain_all.at[g, slot], gc_send.at[g, k], gc_recv.at[g, slot],
            ctx=lax.rem(ctx + k, n_ctx),
        )

    def gt_copy(g, k, slot):
        return remote(
            gain_tp.at[g, slot], gain_tp.at[g, slot], gt_send.at[g, k], gt_recv.at[g, slot],
            tp=lax.rem(tp + k, n_tp),
        )

    def blocks_summed(g):
        each(n_ctx, lambda k: gc_copy(g, k, lax.rem(ctx + k, n_ctx)).wait_recv())
        gain_tp[g, tp] = lax.fori_loop(1, n_ctx, lambda i, t: t + gain_all[g, i], gain_all[g, 0])
        each(n_tp, lambda k: gt_copy(g, k, tp).start())

    macc = jnp.zeros((rows, LANES), F32)
    for g in range(groups):
        for i in range(per_group):
            j = g * per_group + i
            ng[j] = prod[j, pl.ds(pl.multiple_of(tp * rows, rows), rows), :]

            def arrived(d):
                rs_copy(d, tp, j).wait_recv()
                ng[j] = ng[j] + recv[d, tp, j].astype(F32)

            pl.when(tp < n_tp - 1)(functools.partial(arrived, 1))
            pl.when(tp > 0)(functools.partial(arrived, 0))
            vx = ng[j] * xh[j]
            gain_all[g, ctx, pl.ds(i, 1), :] = jnp.sum(fold(vx), 0, keepdims=True)
            macc = macc + fold_lanes(vx * gain_ref[:, slab_cols(j)])
        each(n_ctx, lambda k: gc_copy(g, k, ctx).start())
        if g:
            blocks_summed(g - 1)

    mean = jnp.sum(macc, -1, keepdims=True) / D

    def write(j, _):
        cols = slab_cols(j)
        res = (gain_ref[:, cols] * ng[j] - xh[j] * mean) * inv_v[:, :1]
        out_v[:, cols] = res.astype(BF16)
        return 0

    lax.fori_loop(0, slabs, write, 0)
    out_copy = pltpu.make_async_copy(out_v, out_hbm, out_sem)
    out_copy.start()

    blocks_summed(groups - 1)

    for copy in halos:
        copy.wait_send()
    each(n_ctx, lambda k: tb_copy(k, ctx).wait_send())
    for g in range(groups):
        each(n_ctx, lambda k: gc_copy(g, k, ctx).wait_send())

    for p in range(n_tp - 1):
        for d in range(2):
            r = chunk[d][p]

            @pl.when(sends(d, r))
            def _():
                lax.fori_loop(0, slabs, lambda j, _: (rs_copy(d, r, j).wait_send(), 0)[1], 0)

    for g in range(groups):
        each(n_tp, lambda k: gt_copy(g, k, lax.rem(tp + k, n_tp)).wait_recv())
        gain_sum = sum(gain_tp[g, i] for i in range(n_tp))
        for i in range(per_group):
            j = g * per_group + i
            gain_out[:, j * slab_w:(j + 1) * slab_w] = gain_sum[i:i + 1]
    for g in range(groups):
        each(n_tp, lambda k: gt_copy(g, k, tp).wait_send())
    out_copy.wait()


def publish(*refs):
    for src, dst in zip(refs[:4], refs[4:]):
        dst[...] = src[...]


def on_device(n_ctx, n_tp, hidden_in, norm_gain, proj_weight, conv_in, conv_weight, conv_bias, act_grad):
    T, C = conv_in.shape
    D = proj_weight.shape[0]
    rows = hidden_in.shape[0]
    taps = conv_weight.shape[0]
    slab_w = D // 8
    slabs = D // slab_w
    groups = 4
    hbm = pl.BlockSpec(memory_space=pl.ANY)
    vmem = pl.BlockSpec(memory_space=pltpu.VMEM)
    dma = pltpu.SemaphoreType.DMA
    out_shape = (
        jax.ShapeDtypeStruct((rows, D), BF16),
        jax.ShapeDtypeStruct((1, D), F32),
        jax.ShapeDtypeStruct((taps, C), F32),
        jax.ShapeDtypeStruct((1, C), F32),
    )
    results = pl.pallas_call(
        functools.partial(kernel, n_ctx, n_tp, slab_w),
        out_shape=out_shape,
        in_specs=[hbm] * 7,
        out_specs=(hbm, vmem, vmem, vmem),
        scratch_shapes=[
            pltpu.VMEM((rows, D), BF16),
            pltpu.VMEM((D, C), BF16),
            pltpu.VMEM((T, C), BF16),
            pltpu.VMEM((T, C), BF16),
            pltpu.VMEM((1, D), F32),
            pltpu.VMEM((taps, C), F32),
            pltpu.VMEM((1, C), F32),
            pltpu.VMEM((3, EDGE, C), BF16),
            pltpu.VMEM((T + 2 * PAD, C), F32),
            pltpu.VMEM((T + PAD, C), F32),
            pltpu.VMEM((T - 2 * rows, C), BF16),
            pltpu.VMEM((2 * rows, C), BF16),
            pltpu.VMEM((8, C), F32),
            pltpu.VMEM((slabs, T, slab_w), F32),
            pltpu.VMEM((2, n_tp, slabs, rows, slab_w), BF16),
            pltpu.VMEM((2, n_tp, slabs, rows, slab_w), BF16),
            pltpu.VMEM((slabs, rows, slab_w), F32),
            pltpu.VMEM((slabs, rows, slab_w), F32),
            pltpu.VMEM((rows, LANES), F32),
            pltpu.VMEM((rows, D), BF16),
            pltpu.VMEM((n_ctx, 8, C), F32),
            pltpu.VMEM((groups, n_ctx, slabs // groups, slab_w), F32),
            pltpu.VMEM((groups, n_tp, slabs // groups, slab_w), F32),
            dma((6,)),
            dma((slabs,)),
            dma,
            dma((3,)),
            dma((3,)),
            dma((2, n_tp, slabs)),
            dma((2, n_tp, slabs)),
            dma((n_ctx,)),
            dma((n_ctx,)),
            dma((groups, n_ctx)),
            dma((groups, n_ctx)),
            dma((groups, n_tp)),
            dma((groups, n_tp)),
        ],
        compiler_params=pltpu.CompilerParams(
            collective_id=0, has_side_effects=True, vmem_limit_bytes=60 * 1024 * 1024
        ),
    )(
        hidden_in, norm_gain[None, :], proj_weight, conv_in, conv_weight, conv_bias[None, :], act_grad
    )
    grad, gain, taps_grad, bias_grad = pl.pallas_call(
        publish, out_shape=out_shape, in_specs=[vmem] * 4, out_specs=(vmem,) * 4
    )(*results)
    return grad, gain.reshape(-1), taps_grad, bias_grad.reshape(-1)


def solution(mesh):
    return jax.shard_map(
        functools.partial(on_device, mesh.shape["ctx"], mesh.shape["tp"]),
        mesh=mesh,
        in_specs=(
            P(("ctx", "tp"), None),
            P(),
            P(None, "tp"),
            P("ctx", "tp"),
            P(None, "tp"),
            P("tp"),
            P("ctx", "tp"),
        ),
        out_specs=(P(("ctx", "tp"), None), P(), P(None, "tp"), P("tp")),
        check_vma=False,
    )
```

time: 62.8 us -> 96.9 us (1.54)
  Pallas kernels: 55.8 us -> 96.1 us
  local copies, waits for them, and re-layouts: 5.78 us -> 0 us
    pallas_call x1, Pallas kernels: 55.8 us -> 94.2 us  [on_device(): pl.pallas_call(functools.partial(kernel, n_ctx, n_tp, slab_w), out_shape=...]
    unnamed x4 -> x0, local copies, waits for them, and re-layouts: 5.78 us -> none
    pallas_call x0 -> x1, Pallas kernels: none -> 1.9 us  [on_device(): pl.pallas_call(publish, out_shape=out_shape, in_specs=[vmem] * 4, out_spe...]
where the time goes in v2:
time: 96.9 us; the launch traced here: 96.8 us
  Pallas kernels  96.1 us (99%)
    pallas_call x1, Pallas kernels, on_device(): pl.pallas_call(functools.partial(kernel, n_ctx, n_tp, slab_w), out_shape=...  94.2 us

profile of v2, /device:TPU:0, one launch (start us, length us, event | category | flops | bytes accessed | tf_op | source)
XLA Modules:
  0.0 96.8 jit_solution(15421781602376866887)
XLA Ops:
  0.6 94.2 %shard_map.102 = (bf16[64,4096]{1,0:T(8,128)(2,1)}, f32[1,4096]{1,0:T(1,128)}, f32[4,1024]{1,0:T(4,128)}, f32[1,1024]{1,0:T(1,128)}) custom-call(bf16[64,4096]{1,0:T(8,128)(2,1)} %hid_hbm.1, f32[1,4096]{1,0:T(1,128)} %bitcast.4, bf16[4096,1024]{1,0:T(8,128)(2,1)} %w_hbm.1, bf16[256,1024]{1,0:T(8,128)(2,1)} %x_hbm.1, f32[4,1024]{1,0:T(4,128)} %taps_hbm.1, ...), custom_call_target="tpu_custom_call" | custom-call | tf_op jit(solution)/shard_map/pallas_call | solution.py:379
  94.9 1.9 %shard_map.103 = (bf16[64,4096]{1,0:T(8,128)(2,1)}, f32[1,4096]{1,0:T(1,128)}, f32[4,1024]{1,0:T(4,128)}, f32[1,1024]{1,0:T(1,128)}) custom-call(bf16[64,4096]{1,0:T(8,128)(2,1)} %get-tuple-element.12.refs_0_, f32[1,4096]{1,0:T(1,128)} %get-tuple-element.13.refs_1_, f32[4,1024]{1,0:T(4,128)} %get-tuple-element.14.refs_2_, f32[1,1024]{1,0:T(1,128)} %get-tuple-element.15.refs_3_), custom_call_target="tpu_custom_call" | custom-call | tf_op jit(solution)/shard_map/pallas_call | solution.py:428

commit v3 on v2

--- a/solution.py
+++ b/solution.py
@@ -13,6 +13,8 @@
 LANES = 128
 EDGE = 16
 PAD = 8
+WINDOW = 3
+LAG = 2
 
 
 def chunk_of(rows, most=64):
@@ -156,6 +158,11 @@
             @pl.when(begins[d])
             def _():
                 send[d, r, j] = term(r, j).astype(BF16)
+                if p == 0:
+                    pl.when(j >= WINDOW)(lambda: rs_copy(d, r, j - WINDOW).wait_send())
+                else:
+                    old = jnp.where(j >= WINDOW, r, chunk[d][p - 1])
+                    rs_copy(d, old, lax.rem(j + slabs - WINDOW, slabs)).wait_send()
                 rs_copy(d, r, j).start()
 
     def dot(a, j):
@@ -201,13 +208,6 @@
 
     lax.fori_loop(0, slabs, edge_dot, 0)
 
-    def later_begin(j, _, p=2):
-        begin(p, j)
-        return 0
-
-    for p in range(2, n_tp - 1):
-        lax.fori_loop(0, slabs, functools.partial(later_begin, p=p), 0)
-
     tb[...] = jnp.zeros_like(tb)
 
     def taps_terms(c, _):
@@ -257,22 +257,34 @@
 
     lax.fori_loop(0, slabs, normalise, 0)
 
-    def forward(j, _, p=0):
-        def one(d):
+    def later_begin(j, _, p=2):
+        begin(p, j)
+        return 0
+
+    for p in range(2, n_tp - 1):
+        lax.fori_loop(0, slabs, functools.partial(later_begin, p=p), 0)
+
+    lower = 2 * tp < n_tp
+
+    def forward(i, _, p=0):
+        def one(d, j, now):
             r = chunk[d][p]
 
-            @pl.when(sends(d, r) & jnp.logical_not(begins[d]))
+            @pl.when(now & sends(d, r) & jnp.logical_not(begins[d]))
             def _():
                 rs_copy(d, r, j).wait_recv()
                 send[d, r, j] = (term(r, j) + recv[d, r, j].astype(F32)).astype(BF16)
                 rs_copy(d, r, j).start()
 
-        one(0)
-        one(1)
+        upper = jnp.logical_not(lower)
+        one(0, i, lower & (i < slabs))
+        one(1, i, upper & (i < slabs))
+        one(1, i - LAG, lower & (i >= LAG))
+        one(0, i - LAG, upper & (i >= LAG))
         return 0
 
     for p in range(n_tp - 1):
-        lax.fori_loop(0, slabs, functools.partial(forward, p=p), 0)
+        lax.fori_loop(0, slabs + LAG, functools.partial(forward, p=p), 0)
 
     each(n_ctx, lambda k: tb_copy(k, lax.rem(ctx + k, n_ctx)).wait_recv())
     total = lax.fori_loop(1, n_ctx, lambda i, t: t + tb_all[i], tb_all[0])
@@ -335,11 +347,17 @@
     for g in range(groups):
         each(n_ctx, lambda k: gc_copy(g, k, ctx).wait_send())
 
+    for d in range(2):
+        @pl.when(begins[d])
+        def _():
+            for j in range(slabs - WINDOW, slabs):
+                rs_copy(d, chunk[d][-1], j).wait_send()
+
     for p in range(n_tp - 1):
         for d in range(2):
             r = chunk[d][p]
 
-            @pl.when(sends(d, r))
+            @pl.when(sends(d, r) & jnp.logical_not(begins[d]))
             def _():
                 lax.fori_loop(0, slabs, lambda j, _: (rs_copy(d, r, j).wait_send(), 0)[1], 0)
 

time: 96.9 us -> 57.7 us (0.60)
  Pallas kernels: 96.1 us -> 56.9 us
    pallas_call x1, Pallas kernels: 94.2 us -> 55 us  [on_device(): pl.pallas_call(functools.partial(kernel, n_ctx, n_tp, slab_w), out_shape=...]
where the time goes in v3:
time: 57.7 us; the launch traced here: 57.6 us
  Pallas kernels  56.9 us (99%)
  between operations  0.64 us (1%)
    pallas_call x1, Pallas kernels, on_device(): pl.pallas_call(functools.partial(kernel, n_ctx, n_tp, slab_w), out_shape=...  55 us
    pallas_call x1, Pallas kernels, on_device(): pl.pallas_call(publish, out_shape=out_shape, in_specs=[vmem] * 4, out_spe...  1.9 us

profile of v3, /device:TPU:0, one launch (start us, length us, event | category | flops | bytes accessed | tf_op | source)
XLA Modules:
  0.0 57.6 jit_solution(6549899970969861779)
XLA Ops:
  0.6 55.0 %shard_map.102 = (bf16[64,4096]{1,0:T(8,128)(2,1)}, f32[1,4096]{1,0:T(1,128)}, f32[4,1024]{1,0:T(4,128)}, f32[1,1024]{1,0:T(1,128)}) custom-call(bf16[64,4096]{1,0:T(8,128)(2,1)} %hid_hbm.1, f32[1,4096]{1,0:T(1,128)} %bitcast.4, bf16[4096,1024]{1,0:T(8,128)(2,1)} %w_hbm.1, bf16[256,1024]{1,0:T(8,128)(2,1)} %x_hbm.1, f32[4,1024]{1,0:T(4,128)} %taps_hbm.1, ...), custom_call_target="tpu_custom_call" | custom-call | tf_op jit(solution)/shard_map/pallas_call | solution.py:397
  55.7 1.9 %shard_map.103 = (bf16[64,4096]{1,0:T(8,128)(2,1)}, f32[1,4096]{1,0:T(1,128)}, f32[4,1024]{1,0:T(4,128)}, f32[1,1024]{1,0:T(1,128)}) custom-call(bf16[64,4096]{1,0:T(8,128)(2,1)} %get-tuple-element.12.refs_0_, f32[1,4096]{1,0:T(1,128)} %get-tuple-element.13.refs_1_, f32[4,1024]{1,0:T(4,128)} %get-tuple-element.14.refs_2_, f32[1,1024]{1,0:T(1,128)} %get-tuple-element.15.refs_3_), custom_call_target="tpu_custom_call" | custom-call | tf_op jit(solution)/shard_map/pallas_call | solution.py:446

commit v4 on v3

--- a/solution.py
+++ b/solution.py
@@ -74,11 +74,6 @@
         part = pl.ds(pl.multiple_of(j * slab_w, slab_w), slab_w)
         return pltpu.make_async_copy(w_hbm.at[part], w_v.at[part], w_sem.at[j])
 
-    for j in range(slabs):
-        w_copy(j).start()
-    for copy in inputs[4:]:
-        copy.start()
-
     def remote(src, dst, s_sem, r_sem, **where):
         return pltpu.make_async_remote_copy(
             src_ref=src, dst_ref=dst, send_sem=s_sem, recv_sem=r_sem,
@@ -116,6 +111,10 @@
 
     for copy in inputs[:4]:
         copy.wait()
+    for j in range(slabs):
+        w_copy(j).start()
+    for copy in inputs[4:]:
+        copy.start()
 
     def middle(c, _):
         cols = columns(c)
@@ -161,9 +160,32 @@
                 if p == 0:
                     pl.when(j >= WINDOW)(lambda: rs_copy(d, r, j - WINDOW).wait_send())
                 else:
-                    old = jnp.where(j >= WINDOW, r, chunk[d][p - 1])
-                    rs_copy(d, old, lax.rem(j + slabs - WINDOW, slabs)).wait_send()
+                    earlier = chunk[d][p - 1]
+                    if isinstance(j, int):
+                        old = r if j >= WINDOW else earlier
+                        rs_copy(d, old, (j - WINDOW) % slabs).wait_send()
+                    else:
+                        old = jnp.where(j >= WINDOW, r, earlier)
+                        rs_copy(d, old, lax.rem(j + slabs - WINDOW, slabs)).wait_send()
                 rs_copy(d, r, j).start()
+
+    def pass_on(d, p, j, now=True):
+        r = chunk[d][p]
+
+        @pl.when(now & sends(d, r) & jnp.logical_not(begins[d]))
+        def _():
+            rs_copy(d, r, j).wait_recv()
+            send[d, r, j] = (term(r, j) + recv[d, r, j].astype(F32)).astype(BF16)
+            rs_copy(d, r, j).start()
+
+    def forward(i, _, p=0):
+        lower = 2 * tp < n_tp
+        upper = jnp.logical_not(lower)
+        pass_on(0, p, i, lower & (i < slabs))
+        pass_on(1, p, i, upper & (i < slabs))
+        pass_on(1, p, i - LAG, lower & (i >= LAG))
+        pass_on(0, p, i - LAG, upper & (i >= LAG))
+        return 0
 
     def dot(a, j):
         part = pl.ds(pl.multiple_of(j * slab_w, slab_w), slab_w)
@@ -204,6 +226,8 @@
         prod[j, pl.ds(0, rows), :] = both[:rows]
         prod[j, pl.ds(T - rows, rows), :] = both[rows:]
         begin(1, j)
+        pass_on(0, 0, j)
+        pass_on(1, 0, j)
         return 0
 
     lax.fori_loop(0, slabs, edge_dot, 0)
@@ -261,35 +285,11 @@
         begin(p, j)
         return 0
 
-    for p in range(2, n_tp - 1):
+    for p in range(2, n_tp - 2):
         lax.fori_loop(0, slabs, functools.partial(later_begin, p=p), 0)
 
-    lower = 2 * tp < n_tp
-
-    def forward(i, _, p=0):
-        def one(d, j, now):
-            r = chunk[d][p]
-
-            @pl.when(now & sends(d, r) & jnp.logical_not(begins[d]))
-            def _():
-                rs_copy(d, r, j).wait_recv()
-                send[d, r, j] = (term(r, j) + recv[d, r, j].astype(F32)).astype(BF16)
-                rs_copy(d, r, j).start()
-
-        upper = jnp.logical_not(lower)
-        one(0, i, lower & (i < slabs))
-        one(1, i, upper & (i < slabs))
-        one(1, i - LAG, lower & (i >= LAG))
-        one(0, i - LAG, upper & (i >= LAG))
-        return 0
-
-    for p in range(n_tp - 1):
+    for p in range(1, n_tp - 2):
         lax.fori_loop(0, slabs + LAG, functools.partial(forward, p=p), 0)
-
-    each(n_ctx, lambda k: tb_copy(k, lax.rem(ctx + k, n_ctx)).wait_recv())
-    total = lax.fori_loop(1, n_ctx, lambda i, t: t + tb_all[i], tb_all[0])
-    taps_out[...] = total[:taps]
-    bias_out[...] = total[taps:taps + 1]
 
     def gc_copy(g, k, slot):
         return remote(
@@ -312,6 +312,7 @@
     for g in range(groups):
         for i in range(per_group):
             j = g * per_group + i
+            begin(n_tp - 2, j)
             ng[j] = prod[j, pl.ds(pl.multiple_of(tp * rows, rows), rows), :]
 
             def arrived(d):
@@ -338,6 +339,11 @@
     lax.fori_loop(0, slabs, write, 0)
     out_copy = pltpu.make_async_copy(out_v, out_hbm, out_sem)
     out_copy.start()
+
+    each(n_ctx, lambda k: tb_copy(k, lax.rem(ctx + k, n_ctx)).wait_recv())
+    total = lax.fori_loop(1, n_ctx, lambda i, t: t + tb_all[i], tb_all[0])
+    taps_out[...] = total[:taps]
+    bias_out[...] = total[taps:taps + 1]
 
     blocks_summed(groups - 1)
 

time: 57.7 us -> 55.2 us (0.957)
  Pallas kernels: 56.9 us -> 54.4 us
    pallas_call x1, Pallas kernels: 55 us -> 52.5 us  [on_device(): pl.pallas_call(functools.partial(kernel, n_ctx, n_tp, slab_w), out_shape=...]
where the time goes in v4:
time: 55.2 us; the launch traced here: 55 us
  Pallas kernels  54.4 us (99%)
  between operations  0.64 us (1%)
    pallas_call x1, Pallas kernels, on_device(): pl.pallas_call(functools.partial(kernel, n_ctx, n_tp, slab_w), out_shape=...  52.5 us
    pallas_call x1, Pallas kernels, on_device(): pl.pallas_call(publish, out_shape=out_shape, in_specs=[vmem] * 4, out_spe...  1.9 us

profile of v4, /device:TPU:0, one launch (start us, length us, event | category | flops | bytes accessed | tf_op | source)
XLA Modules:
  0.0 55.0 jit_solution(4385046499609874610)
XLA Ops:
  0.6 52.5 %shard_map.102 = (bf16[64,4096]{1,0:T(8,128)(2,1)}, f32[1,4096]{1,0:T(1,128)}, f32[4,1024]{1,0:T(4,128)}, f32[1,1024]{1,0:T(1,128)}) custom-call(bf16[64,4096]{1,0:T(8,128)(2,1)} %hid_hbm.1, f32[1,4096]{1,0:T(1,128)} %bitcast.4, bf16[4096,1024]{1,0:T(8,128)(2,1)} %w_hbm.1, bf16[256,1024]{1,0:T(8,128)(2,1)} %x_hbm.1, f32[4,1024]{1,0:T(4,128)} %taps_hbm.1, ...), custom_call_target="tpu_custom_call" | custom-call | tf_op jit(solution)/shard_map/pallas_call | solution.py:403
  53.1 1.9 %shard_map.103 = (bf16[64,4096]{1,0:T(8,128)(2,1)}, f32[1,4096]{1,0:T(1,128)}, f32[4,1024]{1,0:T(4,128)}, f32[1,1024]{1,0:T(1,128)}) custom-call(bf16[64,4096]{1,0:T(8,128)(2,1)} %get-tuple-element.12.refs_0_, f32[1,4096]{1,0:T(1,128)} %get-tuple-element.13.refs_1_, f32[4,1024]{1,0:T(4,128)} %get-tuple-element.14.refs_2_, f32[1,1024]{1,0:T(1,128)} %get-tuple-element.15.refs_3_), custom_call_target="tpu_custom_call" | custom-call | tf_op jit(solution)/shard_map/pallas_call | solution.py:452
